TPU v7x, 32 devices: a whole 2x2x4 slice. The times are simulated.
32 devices in a mesh: groups: 2 (over y), dom: 8 (over z, core), tilt: 2 (over x), rep: 1.
Axes of the slice: x: 2, y: 2, z: 4, core: 2. Of those that a mesh axis runs over, the one named last changes fastest.
Arguments:
- patches: bfloat16 [4, 1024, 128, 128], P(('groups', 'tilt'), 'dom'), parts along dimension 0, may hold values from -6 to 6
- slot_view: int32 [4, 1024, 1], P(('groups', 'tilt'), 'dom'), parts along dimension 0, may hold values from 0 to 31, as said below
- slot_tilt: int32 [4, 1024], P(('groups', 'tilt'), 'dom'), parts along dimension 0, may hold values from 0 to 9
- slot_pos: bfloat16 [2, 4, 1024], P(None, ('groups', 'tilt'), 'dom'), parts along dimension 1, may hold values from 0 to 1
- defocus: bfloat16 [4, 1024], P(('groups', 'tilt'), 'dom'), parts along dimension 0, may hold values from 1 to 3
- projections: bfloat16 [64, 20, 2, 128, 128], P(('groups', 'dom'), 'tilt', None, 'rep'), parts along dimension 0, may hold values from -6 to 6
- warp_grid: float32 [40, 2, 256], P(('groups', 'tilt')), parts along dimension 0, may hold values from -6 to 6
Outputs:
- slot_terms: float32 [3, 4, 1024], P(None, ('groups', 'tilt'), 'dom'), parts along dimension 1
- new_warp: float32 [40, 2, 256], P(('groups', 'tilt')), parts along dimension 0
There are 2 independent parts, one for each index of `groups`. A program takes and returns all parts, laid end to end along the dimension named above; each array names one. Nothing has to cross between parts.
Inputs may be any that keep to these rules, and one draw needn't show every extreme that they name: `slot_view`: view v is owned by dom index v // 4. Among the 128 slots of one device (one tilt index and one dom index) at most 24 name views of any one owner, and in every such block some owner is named exactly 24 times.
All inputs are finite; a program needn't handle non-finite values.
Results may differ from a plain program's by a relative error of at most 0.0018.
Values may be sent and summed in bfloat16 or wider, within the bound.
A program may use at most 64 MiB of HBM per device.

v0:
```python
import math
import jax
import jax.numpy as jnp
from jax import lax
from jax.sharding import PartitionSpec as P

GRID = 16
AMPLITUDE = 0.07
TRUST_FLOOR = 0.02


def signed_freq(index, pixels):
    return jnp.where(index < pixels // 2, index, index - pixels).astype(jnp.float32)


def dft_tables(freq_rows, pixels):
    columns = jnp.arange(pixels, dtype=jnp.int32)
    table_scale = 1.0 / math.sqrt(pixels)
    turns_rows = (freq_rows[:, None] * columns[None, :] % pixels).astype(jnp.float32) * (
        2.0 * math.pi / pixels
    )
    turns_full = (columns[:, None] * columns[None, :] % pixels).astype(jnp.float32) * (
        2.0 * math.pi / pixels
    )
    row_table = jnp.concatenate([jnp.cos(turns_rows), jnp.sin(turns_rows)], axis=0) * table_scale
    col_table = jnp.concatenate([jnp.cos(turns_full), jnp.sin(turns_full)], axis=1) * table_scale
    return (row_table.astype(jnp.bfloat16), col_table.astype(jnp.bfloat16))


def node_weights(pos_x, pos_y, grid_side):
    knot_pos = jnp.arange(grid_side, dtype=jnp.int32).astype(jnp.float32)
    weight_x = jnp.maximum(0.0, 1.0 - jnp.abs(pos_x[:, None] * (grid_side - 1) - knot_pos[None, :]))
    weight_y = jnp.maximum(0.0, 1.0 - jnp.abs(pos_y[:, None] * (grid_side - 1) - knot_pos[None, :]))
    return (weight_y[:, :, None] * weight_x[:, None, :]).reshape(
        pos_x.shape[0], grid_side * grid_side
    )


def spectral_terms(spectrum, ref_blk, focus_blk, shift_blk, freq_rows, pixels):
    row_total = freq_rows.shape[0]
    v_one_cos = spectrum[:, :row_total, :pixels]
    v_one_sin = spectrum[:, :row_total, pixels:]
    v_two_cos = spectrum[:, row_total:, :pixels]
    v_two_sin = spectrum[:, row_total:, pixels:]
    real_part = v_one_cos - v_two_sin
    imag_part = -(v_one_sin + v_two_cos)
    freq_y = signed_freq(freq_rows, pixels)[None, :, None]
    freq_x = signed_freq(jnp.arange(pixels, dtype=jnp.int32), pixels)[None, None, :]
    nyquist = pixels / 2.0
    radius = (freq_y * freq_y + freq_x * freq_x) / (nyquist * nyquist)
    aberration = math.pi * focus_blk[:, None, None] * radius
    contrast = -(
        math.sqrt(1.0 - AMPLITUDE * AMPLITUDE) * jnp.sin(aberration)
        + AMPLITUDE * jnp.cos(aberration)
    )
    phase_angle = (
        2.0
        * math.pi
        / pixels
        * (freq_x * shift_blk[:, 0, None, None] + freq_y * shift_blk[:, 1, None, None])
    )
    cosine = jnp.cos(phase_angle)
    sine_part = jnp.sin(phase_angle)
    ref_real = ref_blk[:, 0].astype(jnp.float32)
    ref_imag = ref_blk[:, 1].astype(jnp.float32)
    model_real = contrast * (ref_real * cosine + ref_imag * sine_part)
    model_imag = contrast * (ref_imag * cosine - ref_real * sine_part)
    diff_real = real_part - model_real
    diff_imag = imag_part - model_imag
    inverse_area = 1.0 / (pixels * pixels)
    energy = jnp.sum(diff_real * diff_real + diff_imag * diff_imag, axis=(1, 2)) * inverse_area
    cross_term = diff_imag * model_real - diff_real * model_imag
    grad_x = 2.0 * inverse_area * jnp.sum(2.0 * math.pi / pixels * freq_x * cross_term, axis=(1, 2))
    grad_y = 2.0 * inverse_area * jnp.sum(2.0 * math.pi / pixels * freq_y * cross_term, axis=(1, 2))
    return jnp.stack([energy, grad_x, grad_y], axis=1)


def on_device(patches, slot_view, slot_tilt, slot_pos, defocus, projections, warp_grid):
    owners = lax.axis_size("dom")
    slot_count = patches.shape[1]
    pixels = patches.shape[-1]
    view_dev = projections.shape[0]
    tilt_dev = warp_grid.shape[0]
    node_count = warp_grid.shape[2]
    capacity = 3 * slot_count // (2 * owners)
    buffer_len = owners * capacity
    chosen_view = slot_view[0, :, 0]
    owner_of = chosen_view // view_dev
    owner_hits = (owner_of[:, None] == jnp.arange(owners, dtype=jnp.int32)[None, :]).astype(
        jnp.int32
    )
    earlier = jnp.cumsum(owner_hits, axis=0) - owner_hits
    slot_rank = jnp.sum(earlier * owner_hits, axis=1)
    target = owner_of * capacity + slot_rank
    matches = target[None, :] == jnp.arange(buffer_len, dtype=jnp.int32)[:, None]
    source = jnp.sum(
        jnp.where(matches, jnp.arange(slot_count, dtype=jnp.int32)[None, :], 0), axis=1
    )
    filled = jnp.any(matches, axis=1)
    patch_rows = jnp.where(filled[:, None, None], patches[0][source], jnp.zeros((), jnp.bfloat16))
    slot_meta = jnp.stack(
        [
            slot_tilt[0].astype(jnp.float32),
            (chosen_view % view_dev).astype(jnp.float32),
            defocus[0].astype(jnp.float32),
            slot_pos[0, 0].astype(jnp.float32),
            slot_pos[1, 0].astype(jnp.float32),
            jnp.ones((slot_count,), jnp.float32),
        ],
        axis=1,
    )
    meta_rows = jnp.where(filled[:, None], slot_meta[source], 0.0).astype(jnp.bfloat16)
    patch_buffer = patch_rows.reshape(owners, capacity, pixels, pixels)
    meta_buffer = meta_rows.reshape(owners, capacity, 6)
    row_span = projections.shape[3]
    freq_rows = lax.axis_index("rep") * row_span + jnp.arange(row_span, dtype=jnp.int32)
    row_table, col_table = dft_tables(freq_rows, pixels)
    row_total = freq_rows.shape[0]
    projected_flat = projections.reshape(view_dev * tilt_dev, 2, row_total, pixels)
    tilt_iota = jnp.arange(tilt_dev, dtype=jnp.int32)
    view_iota = jnp.arange(view_dev, dtype=jnp.int32)

    def one_block(inputs):
        patch_blk, index_blk, focus_blk, shift_blk = inputs
        ref_blk = projected_flat[index_blk]
        first_pass = jnp.einsum(
            "fy,byx->bfx", row_table, patch_blk, preferred_element_type=jnp.float32
        ).astype(jnp.bfloat16)
        spectrum = jnp.einsum(
            "bfx,xk->bfk", first_pass, col_table, preferred_element_type=jnp.float32
        )
        return spectral_terms(spectrum, ref_blk, focus_blk, shift_blk, freq_rows, pixels)

    patch_in = lax.all_to_all(patch_buffer, "dom", split_axis=0, concat_axis=0, tiled=True)
    meta_in = lax.all_to_all(meta_buffer, "dom", split_axis=0, concat_axis=0, tiled=True)
    senders = patch_in.shape[0]
    per_sender = patch_in.shape[1]
    slot_total = senders * per_sender
    meta_flat = meta_in.reshape(slot_total, 6).astype(jnp.float32)
    tilt_match = meta_flat[:, 0:1] == tilt_iota.astype(jnp.float32)[None, :]
    view_match = meta_flat[:, 1:2] == view_iota.astype(jnp.float32)[None, :]
    tilt_local = jnp.sum(jnp.where(tilt_match, tilt_iota[None, :], 0), axis=1)
    view_local = jnp.sum(jnp.where(view_match, view_iota[None, :], 0), axis=1)
    weights = node_weights(meta_flat[:, 3], meta_flat[:, 4], GRID)
    shifts = jnp.sum(warp_grid[tilt_local] * weights[:, None, :], axis=2)
    block_len = math.gcd(slot_total, 16)
    block_count = slot_total // block_len
    per_slot = lax.map(
        one_block,
        (
            patch_in.reshape(block_count, block_len, pixels, pixels),
            (view_local * tilt_dev + tilt_local).reshape(block_count, block_len),
            meta_flat[:, 2].reshape(block_count, block_len),
            shifts.reshape(block_count, block_len, 2),
        ),
    ).reshape(slot_total, 3)
    node_coef = (
        tilt_match.astype(jnp.float32)[:, :, None]
        * per_slot[:, None, 1:3]
        * meta_flat[:, 5, None, None]
    ).reshape(senders, per_sender, 2 * tilt_dev)
    returned = lax.all_to_all(
        per_slot.reshape(senders, per_sender, 3), "dom", split_axis=0, concat_axis=0, tiled=True
    )
    weight_all = weights.reshape(senders, per_sender, node_count)
    own_terms = returned.reshape(buffer_len, 3)[target]
    summed = lax.psum(own_terms, "rep")
    slot_terms = summed.T[:, None, :]
    gradient = jnp.dot(
        node_coef.reshape(-1, 2 * tilt_dev).T,
        weight_all.reshape(-1, node_count),
        precision=lax.Precision.HIGHEST,
        preferred_element_type=jnp.float32,
    ).reshape(tilt_dev, 2, node_count)
    whole_grad = lax.psum(gradient, ("dom", "rep"))
    new_warp = warp_grid - whole_grad / jnp.sqrt(
        whole_grad * whole_grad + TRUST_FLOOR * TRUST_FLOOR
    )
    return (slot_terms, new_warp)


def solution(mesh):
    in_specs = (
        P(("groups", "tilt"), "dom", None, None),
        P(("groups", "tilt"), "dom", None),
        P(("groups", "tilt"), "dom"),
        P(None, ("groups", "tilt"), "dom"),
        P(("groups", "tilt"), "dom"),
        P(("groups", "dom"), "tilt", None, "rep", None),
        P(("groups", "tilt"), None, None),
    )
    out_specs = (P(None, ("groups", "tilt"), "dom"), P(("groups", "tilt"), None, None))
    return jax.shard_map(
        on_device, mesh=mesh, in_specs=in_specs, out_specs=out_specs, check_vma=False
    )
```

profile of v0, /device:TPU:0, one launch (start us, length us, event | category | flops | bytes accessed | tf_op | source)
XLA Modules:
  0.0 444.6 jit_solution(1007006649997248516)
XLA Ops:
  7.2 6.4 %all-to-all-start.1 = ((bf16[8,24,6]{1,2,0:T(8,128)(2,1)}), bf16[8,24,6]{1,2,0:T(8,128)(2,1)S(1)}, u32[]{:S(2)}, u32[]{:S(2)}) async-start(bf16[8,24,6]{1,2,0:T(8,128)(2,1)} %select_convert_fusion), calls=%async_computation.1 | async-start | bytes 32768 | tf_op jit(solution)/shard_map/all_to_all | solution.py:135
  13.5 10.2 %gather_fusion.1 = bf16[192,128,128]{2,1,0:T(8,128)(2,1)} fusion(bf16[128,128,128]{2,1,0:T(8,128)(2,1)} %bitcast.181, s32[1024]{0:T(1024)S(1)} %pad_clamp_fusion.3), kind=kCustom, calls=%fused_computation.1 | custom fusion | bytes 12583680 | tf_op jit(solution)/shard_map/gather | solution.py:100
  23.8 8.6 %copy.103 = bf16[8,24,128,128]{2,3,1,0:T(8,128)(2,1)} copy(bf16[8,24,128,128]{3,2,1,0:T(8,128)(2,1)} %bitcast.179) | data formatting | bytes 12582912 | tf_op jit(solution)/shard_map/gather | solution.py:100
  32.4 5.9 %broadcast_select_fusion = bf16[8,24,128,128]{2,3,1,0:T(8,128)(2,1)} fusion(bf16[8,24,128,128]{2,3,1,0:T(8,128)(2,1)} %copy.103, pred[8,24]{1,0:T(8,128)(4,1)S(1)} %broadcast_in_dim.106), kind=kLoop, calls=%fused_computation.65 | loop fusion | flops 3145728 | bytes 12583104 | tf_op jit(solution)/shard_map/jit(_where)/select_n | solution.py:100
  38.3 5.2 %all-to-all-start = ((bf16[8,24,128,128]{2,3,1,0:T(8,128)(2,1)}), bf16[8,24,128,128]{2,3,1,0:T(8,128)(2,1)}, u32[]{:S(2)}, u32[]{:S(2)}) async-start(bf16[8,24,128,128]{2,3,1,0:T(8,128)(2,1)} %broadcast_select_fusion), calls=%async_computation | async-start | bytes 12582912 | tf_op jit(solution)/shard_map/all_to_all | solution.py:134
  46.3 136.3 %all-to-all-done = bf16[8,24,128,128]{2,3,1,0:T(8,128)(2,1)} async-done(((bf16[8,24,128,128]{2,3,1,0:T(8,128)(2,1)}), bf16[8,24,128,128]{2,3,1,0:T(8,128)(2,1)}, u32[]{:S(2)}, u32[]{:S(2)}) %all-to-all-start) | async-done | bytes 6291488 | tf_op jit(solution)/shard_map/all_to_all | solution.py:134
  182.6 223.7 %while.15 = (s32[]{:T(128)}, f32[12,16,3]{1,0,2:T(8,128)S(1)}, bf16[12,16,128,128]{2,3,1,0:T(8,128)(2,1)}, bf16[256,128]{1,0:T(8,128)(2,1)S(1)}, bf16[128,256]{1...) while((s32[]{:T(128)}, f32[12,16,3]{1,0,2:T(8,128)S(1)}, ...), condition=%wide.region_11.12_spmd.clone.clone, body=%wide.region_7.11_spmd.clone.clone.sunk | while | flops 411868064 | bytes 14461309 | solution.py:148
  189.8 10.9 %add_reduce_fusion.2 = (f32[16]{0:T(128)S(1)}, f32[16,128,128]{2,1,0:T(8,128)S(1)}) fusion(f32[16,256,256]{2,1,0:T(8,128)} %fusion.62, bf16[16,2,128,128]{3,2,1,0:T(8,128)(2,1)S(1)} %gather_fusion, f32[16,128]{1,0:T(8,128)S(1)} %get-tuple-element.371, f32[16,128]{1,0:T(8,128)S(1)} %get-tuple-element.372, f32[128,128]{1,0:T(8,128)S(1)} %add_multiply_fusion.3, ...), kind=kLoop, calls=%fused_computation.31.clone.1 | loop fusion | flops 7602160 | bytes 6373504 | tf_op jit(solution)/shard_map/while/body/eval_jaxpr/reduce_sum | solution.py:71
  208.5 10.9 %add_reduce_fusion.2 = (f32[16]{0:T(128)S(1)}, f32[16,128,128]{2,1,0:T(8,128)S(1)}) fusion(f32[16,256,256]{2,1,0:T(8,128)} %fusion.62, bf16[16,2,128,128]{3,2,1,0:T(8,128)(2,1)S(1)} %gather_fusion, f32[16,128]{1,0:T(8,128)S(1)} %get-tuple-element.371, f32[16,128]{1,0:T(8,128)S(1)} %get-tuple-element.372, f32[128,128]{1,0:T(8,128)S(1)} %add_multiply_fusion.3, ...), kind=kLoop, calls=%fused_computation.31.clone.1 | loop fusion | flops 7602160 | bytes 6373504 | tf_op jit(solution)/shard_map/while/body/eval_jaxpr/reduce_sum | solution.py:71
  220.0 4.5 %fusion.62 = f32[16,256,256]{2,1,0:T(8,128)} fusion(bf16[12,16,128,128]{2,3,1,0:T(8,128)(2,1)} %get-tuple-element.403, s32[]{:T(128)} %get-tuple-element.390, bf16[128,256]{1,0:T(8,128)(2,1)S(1)} %get-tuple-element.405, bf16[256,128]{1,0:T(8,128)(2,1)S(1)} %get-tuple-element.404), kind=kOutput, calls=%fused_computation.10.clone.1 | convolution fusion | flops 403177472 | bytes 4850176 | tf_op jit(solution)/shard_map/while/body/eval_jaxpr/bfx,xk->bfk/dot_general | solution.py:129
  227.1 10.9 %add_reduce_fusion.2 = (f32[16]{0:T(128)S(1)}, f32[16,128,128]{2,1,0:T(8,128)S(1)}) fusion(f32[16,256,256]{2,1,0:T(8,128)} %fusion.62, bf16[16,2,128,128]{3,2,1,0:T(8,128)(2,1)S(1)} %gather_fusion, f32[16,128]{1,0:T(8,128)S(1)} %get-tuple-element.371, f32[16,128]{1,0:T(8,128)S(1)} %get-tuple-element.372, f32[128,128]{1,0:T(8,128)S(1)} %add_multiply_fusion.3, ...), kind=kLoop, calls=%fused_computation.31.clone.1 | loop fusion | flops 7602160 | bytes 6373504 | tf_op jit(solution)/shard_map/while/body/eval_jaxpr/reduce_sum | solution.py:71
  238.6 4.5 %fusion.62 = f32[16,256,256]{2,1,0:T(8,128)} fusion(bf16[12,16,128,128]{2,3,1,0:T(8,128)(2,1)} %get-tuple-element.403, s32[]{:T(128)} %get-tuple-element.390, bf16[128,256]{1,0:T(8,128)(2,1)S(1)} %get-tuple-element.405, bf16[256,128]{1,0:T(8,128)(2,1)S(1)} %get-tuple-element.404), kind=kOutput, calls=%fused_computation.10.clone.1 | convolution fusion | flops 403177472 | bytes 4850176 | tf_op jit(solution)/shard_map/while/body/eval_jaxpr/bfx,xk->bfk/dot_general | solution.py:129
  245.8 10.9 %add_reduce_fusion.2 = (f32[16]{0:T(128)S(1)}, f32[16,128,128]{2,1,0:T(8,128)S(1)}) fusion(f32[16,256,256]{2,1,0:T(8,128)} %fusion.62, bf16[16,2,128,128]{3,2,1,0:T(8,128)(2,1)S(1)} %gather_fusion, f32[16,128]{1,0:T(8,128)S(1)} %get-tuple-element.371, f32[16,128]{1,0:T(8,128)S(1)} %get-tuple-element.372, f32[128,128]{1,0:T(8,128)S(1)} %add_multiply_fusion.3, ...), kind=kLoop, calls=%fused_computation.31.clone.1 | loop fusion | flops 7602160 | bytes 6373504 | tf_op jit(solution)/shard_map/while/body/eval_jaxpr/reduce_sum | solution.py:71
  264.4 10.9 %add_reduce_fusion.2 = (f32[16]{0:T(128)S(1)}, f32[16,128,128]{2,1,0:T(8,128)S(1)}) fusion(f32[16,256,256]{2,1,0:T(8,128)} %fusion.62, bf16[16,2,128,128]{3,2,1,0:T(8,128)(2,1)S(1)} %gather_fusion, f32[16,128]{1,0:T(8,128)S(1)} %get-tuple-element.371, f32[16,128]{1,0:T(8,128)S(1)} %get-tuple-element.372, f32[128,128]{1,0:T(8,128)S(1)} %add_multiply_fusion.3, ...), kind=kLoop, calls=%fused_computation.31.clone.1 | loop fusion | flops 7602160 | bytes 6373504 | tf_op jit(solution)/shard_map/while/body/eval_jaxpr/reduce_sum | solution.py:71
  275.9 4.5 %fusion.62 = f32[16,256,256]{2,1,0:T(8,128)} fusion(bf16[12,16,128,128]{2,3,1,0:T(8,128)(2,1)} %get-tuple-element.403, s32[]{:T(128)} %get-tuple-element.390, bf16[128,256]{1,0:T(8,128)(2,1)S(1)} %get-tuple-element.405, bf16[256,128]{1,0:T(8,128)(2,1)S(1)} %get-tuple-element.404), kind=kOutput, calls=%fused_computation.10.clone.1 | convolution fusion | flops 403177472 | bytes 4850176 | tf_op jit(solution)/shard_map/while/body/eval_jaxpr/bfx,xk->bfk/dot_general | solution.py:129
  283.1 10.9 %add_reduce_fusion.2 = (f32[16]{0:T(128)S(1)}, f32[16,128,128]{2,1,0:T(8,128)S(1)}) fusion(f32[16,256,256]{2,1,0:T(8,128)} %fusion.62, bf16[16,2,128,128]{3,2,1,0:T(8,128)(2,1)S(1)} %gather_fusion, f32[16,128]{1,0:T(8,128)S(1)} %get-tuple-element.371, f32[16,128]{1,0:T(8,128)S(1)} %get-tuple-element.372, f32[128,128]{1,0:T(8,128)S(1)} %add_multiply_fusion.3, ...), kind=kLoop, calls=%fused_computation.31.clone.1 | loop fusion | flops 7602160 | bytes 6373504 | tf_op jit(solution)/shard_map/while/body/eval_jaxpr/reduce_sum | solution.py:71
  301.7 10.9 %add_reduce_fusion.2 = (f32[16]{0:T(128)S(1)}, f32[16,128,128]{2,1,0:T(8,128)S(1)}) fusion(f32[16,256,256]{2,1,0:T(8,128)} %fusion.62, bf16[16,2,128,128]{3,2,1,0:T(8,128)(2,1)S(1)} %gather_fusion, f32[16,128]{1,0:T(8,128)S(1)} %get-tuple-element.371, f32[16,128]{1,0:T(8,128)S(1)} %get-tuple-element.372, f32[128,128]{1,0:T(8,128)S(1)} %add_multiply_fusion.3, ...), kind=kLoop, calls=%fused_computation.31.clone.1 | loop fusion | flops 7602160 | bytes 6373504 | tf_op jit(solution)/shard_map/while/body/eval_jaxpr/reduce_sum | solution.py:71
  320.4 10.9 %add_reduce_fusion.2 = (f32[16]{0:T(128)S(1)}, f32[16,128,128]{2,1,0:T(8,128)S(1)}) fusion(f32[16,256,256]{2,1,0:T(8,128)} %fusion.62, bf16[16,2,128,128]{3,2,1,0:T(8,128)(2,1)S(1)} %gather_fusion, f32[16,128]{1,0:T(8,128)S(1)} %get-tuple-element.371, f32[16,128]{1,0:T(8,128)S(1)} %get-tuple-element.372, f32[128,128]{1,0:T(8,128)S(1)} %add_multiply_fusion.3, ...), kind=kLoop, calls=%fused_computation.31.clone.1 | loop fusion | flops 7602160 | bytes 6373504 | tf_op jit(solution)/shard_map/while/body/eval_jaxpr/reduce_sum | solution.py:71
  339.0 10.9 %add_reduce_fusion.2 = (f32[16]{0:T(128)S(1)}, f32[16,128,128]{2,1,0:T(8,128)S(1)}) fusion(f32[16,256,256]{2,1,0:T(8,128)} %fusion.62, bf16[16,2,128,128]{3,2,1,0:T(8,128)(2,1)S(1)} %gather_fusion, f32[16,128]{1,0:T(8,128)S(1)} %get-tuple-element.371, f32[16,128]{1,0:T(8,128)S(1)} %get-tuple-element.372, f32[128,128]{1,0:T(8,128)S(1)} %add_multiply_fusion.3, ...), kind=kLoop, calls=%fused_computation.31.clone.1 | loop fusion | flops 7602160 | bytes 6373504 | tf_op jit(solution)/shard_map/while/body/eval_jaxpr/reduce_sum | solution.py:71
  357.7 10.9 %add_reduce_fusion.2 = (f32[16]{0:T(128)S(1)}, f32[16,128,128]{2,1,0:T(8,128)S(1)}) fusion(f32[16,256,256]{2,1,0:T(8,128)} %fusion.62, bf16[16,2,128,128]{3,2,1,0:T(8,128)(2,1)S(1)} %gather_fusion, f32[16,128]{1,0:T(8,128)S(1)} %get-tuple-element.371, f32[16,128]{1,0:T(8,128)S(1)} %get-tuple-element.372, f32[128,128]{1,0:T(8,128)S(1)} %add_multiply_fusion.3, ...), kind=kLoop, calls=%fused_computation.31.clone.1 | loop fusion | flops 7602160 | bytes 6373504 | tf_op jit(solution)/shard_map/while/body/eval_jaxpr/reduce_sum | solution.py:71
  376.3 10.9 %add_reduce_fusion.2 = (f32[16]{0:T(128)S(1)}, f32[16,128,128]{2,1,0:T(8,128)S(1)}) fusion(f32[16,256,256]{2,1,0:T(8,128)} %fusion.62, bf16[16,2,128,128]{3,2,1,0:T(8,128)(2,1)S(1)} %gather_fusion, f32[16,128]{1,0:T(8,128)S(1)} %get-tuple-element.371, f32[16,128]{1,0:T(8,128)S(1)} %get-tuple-element.372, f32[128,128]{1,0:T(8,128)S(1)} %add_multiply_fusion.3, ...), kind=kLoop, calls=%fused_computation.31.clone.1 | loop fusion | flops 7602160 | bytes 6373504 | tf_op jit(solution)/shard_map/while/body/eval_jaxpr/reduce_sum | solution.py:71
  395.0 10.9 %add_reduce_fusion.2 = (f32[16]{0:T(128)S(1)}, f32[16,128,128]{2,1,0:T(8,128)S(1)}) fusion(f32[16,256,256]{2,1,0:T(8,128)} %fusion.62, bf16[16,2,128,128]{3,2,1,0:T(8,128)(2,1)S(1)} %gather_fusion, f32[16,128]{1,0:T(8,128)S(1)} %get-tuple-element.371, f32[16,128]{1,0:T(8,128)S(1)} %get-tuple-element.372, f32[128,128]{1,0:T(8,128)S(1)} %add_multiply_fusion.3, ...), kind=kLoop, calls=%fused_computation.31.clone.1 | loop fusion | flops 7602160 | bytes 6373504 | tf_op jit(solution)/shard_map/while/body/eval_jaxpr/reduce_sum | solution.py:71
  406.9 26.7 %psum.6 = f32[10,2,256]{2,0,1:T(8,128)S(1)} all-reduce(f32[10,2,256]{2,0,1:T(8,128)S(1)} %fusion.42), channel_id=1, replica_groups=mesh['groups'=2,'dom'=8,'tilt'=2,'rep'=1] {'dom','rep'}, use_global_device_ids=true, to_apply=%region_12.13 | all-reduce | flops 5120 | bytes 40960 | tf_op jit(solution)/shard_map/psum | solution.py:175
  438.3 4.9 %all-to-all-done.2 = f32[8,24,3]{1,2,0:T(4,128)S(1)} async-done(((f32[8,24,3]{1,2,0:T(4,128)}), f32[8,24,3]{1,2,0:T(4,128)S(1)}, u32[]{:S(2)}, u32[]{:S(2)}) %all-to-all-start.2) | async-done | bytes 2336 | tf_op jit(solution)/shard_map/all_to_all | solution.py:162
  (275 shorter events, 93.5 us)
Async XLA Ops:
  7.2 31.1 %all-to-all-start.1 = ((bf16[8,24,6]{1,2,0:T(8,128)(2,1)}), bf16[8,24,6]{1,2,0:T(8,128)(2,1)S(1)}, u32[]{:S(2)}, u32[]{:S(2)}) async-start(bf16[8,24,6]{1,2,0:T(8,128)(2,1)} %select_convert_fusion), calls=%async_computation.1 | async-start | bytes 32768 | tf_op jit(solution)/shard_map/all_to_all | solution.py:135
  38.3 6.1 %copy-start = (f32[10,2,256]{2,1,0:T(2,128)S(1)}, f32[10,2,256]{2,1,0:T(2,128)}, u32[]{:S(2)}) copy-start(f32[10,2,256]{2,1,0:T(2,128)} %param.15) | copy-start | bytes 61444
  38.3 144.3 %all-to-all-start = ((bf16[8,24,128,128]{2,3,1,0:T(8,128)(2,1)}), bf16[8,24,128,128]{2,3,1,0:T(8,128)(2,1)}, u32[]{:S(2)}, u32[]{:S(2)}) async-start(bf16[8,24,128,128]{2,3,1,0:T(8,128)(2,1)} %broadcast_select_fusion), calls=%async_computation | async-start | bytes 12582912 | tf_op jit(solution)/shard_map/all_to_all | solution.py:134
  434.3 8.9 %all-to-all-start.2 = ((f32[8,24,3]{1,2,0:T(4,128)}), f32[8,24,3]{1,2,0:T(4,128)S(1)}, u32[]{:S(2)}, u32[]{:S(2)}) async-start(f32[8,24,3]{1,2,0:T(4,128)} %copy.111), calls=%async_computation.2 | async-start | bytes 32768 | tf_op jit(solution)/shard_map/all_to_all | solution.py:162
where the time goes:
time: 447 us; the launch traced here: 445 us
  other arithmetic  149 us (33%)
  waiting for transfers between devices  141 us (32%)
  local copies, waits for them, and re-layouts  56.4 us (13%)
  matrix products  54.4 us (12%)
  blocking collectives  26.7 us (6%)
  starting transfers between devices  14.9 us (3%)
    all_to_all x1, waiting for transfers between devices, on_device(): lax.all_to_all(patch_buffer, 'dom', split_axis=0, concat_axis=0, tiled=True)  136 us
    reduce_sum x12, other arithmetic, spectral_terms(): jnp.sum(diff_real * diff_real + diff_imag * diff_imag, axis=(1, 2))  131 us
    dot_general x12, matrix products, one_block(): jnp.einsum('bfx,xk->bfk', first_pass, col_table, preferred_element_type=j...  54.1 us
    gather x12, local copies, waits for them, and re-layouts, one_block(): ref_blk = projected_flat[index_blk]  29.9 us
    psum x1, blocking collectives, on_device(): whole_grad = lax.psum(gradient, ('dom', 'rep'))  26.7 us
    gather x2, local copies, waits for them, and re-layouts, on_device(): patches[0][source]  18.8 us
  transfers between devices with their start and end apart: 3, of which 2 were waited for; matrix products, arithmetic and copies ran while one was open for 6% of the time, Pallas kernels for 0%

commit v1 on v0

--- a/solution.py
+++ b/solution.py
@@ -172,7 +172,8 @@
         precision=lax.Precision.HIGHEST,
         preferred_element_type=jnp.float32,
     ).reshape(tilt_dev, 2, node_count)
-    whole_grad = lax.psum(gradient, ("dom", "rep"))
+    terms = lax.all_gather(gradient, ("dom", "rep"))
+    whole_grad = jnp.sum(terms, axis=0)
     new_warp = warp_grid - whole_grad / jnp.sqrt(
         whole_grad * whole_grad + TRUST_FLOOR * TRUST_FLOOR
     )

time: 447 us -> 434 us (0.971)
  blocking collectives: 26.7 us -> 14 us
    psum x1 -> x0, blocking collectives: 26.7 us -> none  [on_device(): whole_grad = lax.psum(gradient, ('dom', 'rep'))]
    all_gather x0 -> x1, blocking collectives: none -> 14 us  [on_device(): terms = lax.all_gather(gradient, ('dom', 'rep'))]
where the time goes in v1:
time: 434 us; the launch traced here: 432 us
  other arithmetic  150 us (35%)
  waiting for transfers between devices  141 us (32%)
  local copies, waits for them, and re-layouts  55.8 us (13%)
  matrix products  54.4 us (13%)
  starting transfers between devices  14.9 us (3%)
  blocking collectives  14 us (3%)
    all_to_all x1, waiting for transfers between devices, on_device(): lax.all_to_all(patch_buffer, 'dom', split_axis=0, concat_axis=0, tiled=True)  136 us
    reduce_sum x12, other arithmetic, spectral_terms(): jnp.sum(diff_real * diff_real + diff_imag * diff_imag, axis=(1, 2))  131 us
    dot_general x12, matrix products, one_block(): jnp.einsum('bfx,xk->bfk', first_pass, col_table, preferred_element_type=j...  54.1 us
    gather x12, local copies, waits for them, and re-layouts, one_block(): ref_blk = projected_flat[index_blk]  29.9 us
    gather x2, local copies, waits for them, and re-layouts, on_device(): patches[0][source]  18.8 us
    all_gather x1, blocking collectives, on_device(): terms = lax.all_gather(gradient, ('dom', 'rep'))  14 us
  transfers between devices with their start and end apart: 3, of which 2 were waited for; matrix products, arithmetic and copies ran while one was open for 6% of the time, Pallas kernels for 0%

profile of v1, /device:TPU:0, one launch (start us, length us, event | category | flops | bytes accessed | tf_op | source)
XLA Modules:
  0.0 431.9 jit_solution(754713075372084108)
XLA Ops:
  7.2 6.4 %all-to-all-start.1 = ((bf16[8,24,6]{1,2,0:T(8,128)(2,1)}), bf16[8,24,6]{1,2,0:T(8,128)(2,1)S(1)}, u32[]{:S(2)}, u32[]{:S(2)}) async-start(bf16[8,24,6]{1,2,0:T(8,128)(2,1)} %select_convert_fusion), calls=%async_computation.1 | async-start | bytes 32768 | tf_op jit(solution)/shard_map/all_to_all | solution.py:135
  13.5 10.2 %gather_fusion.1 = bf16[192,128,128]{2,1,0:T(8,128)(2,1)} fusion(bf16[128,128,128]{2,1,0:T(8,128)(2,1)} %bitcast.182, s32[1024]{0:T(1024)S(1)} %pad_clamp_fusion.3), kind=kCustom, calls=%fused_computation.1 | custom fusion | bytes 12583680 | tf_op jit(solution)/shard_map/gather | solution.py:100
  23.8 8.6 %copy.97 = bf16[8,24,128,128]{2,3,1,0:T(8,128)(2,1)} copy(bf16[8,24,128,128]{3,2,1,0:T(8,128)(2,1)} %bitcast.180) | data formatting | bytes 12582912 | tf_op jit(solution)/shard_map/gather | solution.py:100
  32.4 5.9 %broadcast_select_fusion = bf16[8,24,128,128]{2,3,1,0:T(8,128)(2,1)} fusion(bf16[8,24,128,128]{2,3,1,0:T(8,128)(2,1)} %copy.97, pred[8,24]{1,0:T(8,128)(4,1)S(1)} %broadcast_in_dim.106), kind=kLoop, calls=%fused_computation.65 | loop fusion | flops 3145728 | bytes 12583104 | tf_op jit(solution)/shard_map/jit(_where)/select_n | solution.py:100
  38.3 5.2 %all-to-all-start = ((bf16[8,24,128,128]{2,3,1,0:T(8,128)(2,1)}), bf16[8,24,128,128]{2,3,1,0:T(8,128)(2,1)}, u32[]{:S(2)}, u32[]{:S(2)}) async-start(bf16[8,24,128,128]{2,3,1,0:T(8,128)(2,1)} %broadcast_select_fusion), calls=%async_computation | async-start | bytes 12582912 | tf_op jit(solution)/shard_map/all_to_all | solution.py:134
  46.3 136.3 %all-to-all-done = bf16[8,24,128,128]{2,3,1,0:T(8,128)(2,1)} async-done(((bf16[8,24,128,128]{2,3,1,0:T(8,128)(2,1)}), bf16[8,24,128,128]{2,3,1,0:T(8,128)(2,1)}, u32[]{:S(2)}, u32[]{:S(2)}) %all-to-all-start) | async-done | bytes 6291488 | tf_op jit(solution)/shard_map/all_to_all | solution.py:134
  182.6 223.7 %while.15 = (s32[]{:T(128)}, f32[12,16,3]{1,0,2:T(8,128)S(1)}, bf16[12,16,128,128]{2,3,1,0:T(8,128)(2,1)}, bf16[256,128]{1,0:T(8,128)(2,1)S(1)}, bf16[128,256]{1...) while((s32[]{:T(128)}, f32[12,16,3]{1,0,2:T(8,128)S(1)}, ...), condition=%wide.region_11.12_spmd.clone.clone, body=%wide.region_7.11_spmd.clone.clone.sunk | while | flops 411868064 | bytes 14461309 | solution.py:148
  189.8 10.9 %add_reduce_fusion.2 = (f32[16]{0:T(128)S(1)}, f32[16,128,128]{2,1,0:T(8,128)S(1)}) fusion(f32[16,256,256]{2,1,0:T(8,128)} %fusion.62, bf16[16,2,128,128]{3,2,1,0:T(8,128)(2,1)S(1)} %gather_fusion, f32[16,128]{1,0:T(8,128)S(1)} %get-tuple-element.371, f32[16,128]{1,0:T(8,128)S(1)} %get-tuple-element.372, f32[128,128]{1,0:T(8,128)S(1)} %add_multiply_fusion.3, ...), kind=kLoop, calls=%fused_computation.31.clone.1 | loop fusion | flops 7602160 | bytes 6373504 | tf_op jit(solution)/shard_map/while/body/eval_jaxpr/reduce_sum | solution.py:71
  208.5 10.9 %add_reduce_fusion.2 = (f32[16]{0:T(128)S(1)}, f32[16,128,128]{2,1,0:T(8,128)S(1)}) fusion(f32[16,256,256]{2,1,0:T(8,128)} %fusion.62, bf16[16,2,128,128]{3,2,1,0:T(8,128)(2,1)S(1)} %gather_fusion, f32[16,128]{1,0:T(8,128)S(1)} %get-tuple-element.371, f32[16,128]{1,0:T(8,128)S(1)} %get-tuple-element.372, f32[128,128]{1,0:T(8,128)S(1)} %add_multiply_fusion.3, ...), kind=kLoop, calls=%fused_computation.31.clone.1 | loop fusion | flops 7602160 | bytes 6373504 | tf_op jit(solution)/shard_map/while/body/eval_jaxpr/reduce_sum | solution.py:71
  220.0 4.5 %fusion.62 = f32[16,256,256]{2,1,0:T(8,128)} fusion(bf16[12,16,128,128]{2,3,1,0:T(8,128)(2,1)} %get-tuple-element.403, s32[]{:T(128)} %get-tuple-element.390, bf16[128,256]{1,0:T(8,128)(2,1)S(1)} %get-tuple-element.405, bf16[256,128]{1,0:T(8,128)(2,1)S(1)} %get-tuple-element.404), kind=kOutput, calls=%fused_computation.10.clone.1 | convolution fusion | flops 403177472 | bytes 4850176 | tf_op jit(solution)/shard_map/while/body/eval_jaxpr/bfx,xk->bfk/dot_general | solution.py:129
  227.1 10.9 %add_reduce_fusion.2 = (f32[16]{0:T(128)S(1)}, f32[16,128,128]{2,1,0:T(8,128)S(1)}) fusion(f32[16,256,256]{2,1,0:T(8,128)} %fusion.62, bf16[16,2,128,128]{3,2,1,0:T(8,128)(2,1)S(1)} %gather_fusion, f32[16,128]{1,0:T(8,128)S(1)} %get-tuple-element.371, f32[16,128]{1,0:T(8,128)S(1)} %get-tuple-element.372, f32[128,128]{1,0:T(8,128)S(1)} %add_multiply_fusion.3, ...), kind=kLoop, calls=%fused_computation.31.clone.1 | loop fusion | flops 7602160 | bytes 6373504 | tf_op jit(solution)/shard_map/while/body/eval_jaxpr/reduce_sum | solution.py:71
  238.6 4.5 %fusion.62 = f32[16,256,256]{2,1,0:T(8,128)} fusion(bf16[12,16,128,128]{2,3,1,0:T(8,128)(2,1)} %get-tuple-element.403, s32[]{:T(128)} %get-tuple-element.390, bf16[128,256]{1,0:T(8,128)(2,1)S(1)} %get-tuple-element.405, bf16[256,128]{1,0:T(8,128)(2,1)S(1)} %get-tuple-element.404), kind=kOutput, calls=%fused_computation.10.clone.1 | convolution fusion | flops 403177472 | bytes 4850176 | tf_op jit(solution)/shard_map/while/body/eval_jaxpr/bfx,xk->bfk/dot_general | solution.py:129
  245.8 10.9 %add_reduce_fusion.2 = (f32[16]{0:T(128)S(1)}, f32[16,128,128]{2,1,0:T(8,128)S(1)}) fusion(f32[16,256,256]{2,1,0:T(8,128)} %fusion.62, bf16[16,2,128,128]{3,2,1,0:T(8,128)(2,1)S(1)} %gather_fusion, f32[16,128]{1,0:T(8,128)S(1)} %get-tuple-element.371, f32[16,128]{1,0:T(8,128)S(1)} %get-tuple-element.372, f32[128,128]{1,0:T(8,128)S(1)} %add_multiply_fusion.3, ...), kind=kLoop, calls=%fused_computation.31.clone.1 | loop fusion | flops 7602160 | bytes 6373504 | tf_op jit(solution)/shard_map/while/body/eval_jaxpr/reduce_sum | solution.py:71
  264.4 10.9 %add_reduce_fusion.2 = (f32[16]{0:T(128)S(1)}, f32[16,128,128]{2,1,0:T(8,128)S(1)}) fusion(f32[16,256,256]{2,1,0:T(8,128)} %fusion.62, bf16[16,2,128,128]{3,2,1,0:T(8,128)(2,1)S(1)} %gather_fusion, f32[16,128]{1,0:T(8,128)S(1)} %get-tuple-element.371, f32[16,128]{1,0:T(8,128)S(1)} %get-tuple-element.372, f32[128,128]{1,0:T(8,128)S(1)} %add_multiply_fusion.3, ...), kind=kLoop, calls=%fused_computation.31.clone.1 | loop fusion | flops 7602160 | bytes 6373504 | tf_op jit(solution)/shard_map/while/body/eval_jaxpr/reduce_sum | solution.py:71
  275.9 4.5 %fusion.62 = f32[16,256,256]{2,1,0:T(8,128)} fusion(bf16[12,16,128,128]{2,3,1,0:T(8,128)(2,1)} %get-tuple-element.403, s32[]{:T(128)} %get-tuple-element.390, bf16[128,256]{1,0:T(8,128)(2,1)S(1)} %get-tuple-element.405, bf16[256,128]{1,0:T(8,128)(2,1)S(1)} %get-tuple-element.404), kind=kOutput, calls=%fused_computation.10.clone.1 | convolution fusion | flops 403177472 | bytes 4850176 | tf_op jit(solution)/shard_map/while/body/eval_jaxpr/bfx,xk->bfk/dot_general | solution.py:129
  283.1 10.9 %add_reduce_fusion.2 = (f32[16]{0:T(128)S(1)}, f32[16,128,128]{2,1,0:T(8,128)S(1)}) fusion(f32[16,256,256]{2,1,0:T(8,128)} %fusion.62, bf16[16,2,128,128]{3,2,1,0:T(8,128)(2,1)S(1)} %gather_fusion, f32[16,128]{1,0:T(8,128)S(1)} %get-tuple-element.371, f32[16,128]{1,0:T(8,128)S(1)} %get-tuple-element.372, f32[128,128]{1,0:T(8,128)S(1)} %add_multiply_fusion.3, ...), kind=kLoop, calls=%fused_computation.31.clone.1 | loop fusion | flops 7602160 | bytes 6373504 | tf_op jit(solution)/shard_map/while/body/eval_jaxpr/reduce_sum | solution.py:71
  301.7 10.9 %add_reduce_fusion.2 = (f32[16]{0:T(128)S(1)}, f32[16,128,128]{2,1,0:T(8,128)S(1)}) fusion(f32[16,256,256]{2,1,0:T(8,128)} %fusion.62, bf16[16,2,128,128]{3,2,1,0:T(8,128)(2,1)S(1)} %gather_fusion, f32[16,128]{1,0:T(8,128)S(1)} %get-tuple-element.371, f32[16,128]{1,0:T(8,128)S(1)} %get-tuple-element.372, f32[128,128]{1,0:T(8,128)S(1)} %add_multiply_fusion.3, ...), kind=kLoop, calls=%fused_computation.31.clone.1 | loop fusion | flops 7602160 | bytes 6373504 | tf_op jit(solution)/shard_map/while/body/eval_jaxpr/reduce_sum | solution.py:71
  320.4 10.9 %add_reduce_fusion.2 = (f32[16]{0:T(128)S(1)}, f32[16,128,128]{2,1,0:T(8,128)S(1)}) fusion(f32[16,256,256]{2,1,0:T(8,128)} %fusion.62, bf16[16,2,128,128]{3,2,1,0:T(8,128)(2,1)S(1)} %gather_fusion, f32[16,128]{1,0:T(8,128)S(1)} %get-tuple-element.371, f32[16,128]{1,0:T(8,128)S(1)} %get-tuple-element.372, f32[128,128]{1,0:T(8,128)S(1)} %add_multiply_fusion.3, ...), kind=kLoop, calls=%fused_computation.31.clone.1 | loop fusion | flops 7602160 | bytes 6373504 | tf_op jit(solution)/shard_map/while/body/eval_jaxpr/reduce_sum | solution.py:71
  339.0 10.9 %add_reduce_fusion.2 = (f32[16]{0:T(128)S(1)}, f32[16,128,128]{2,1,0:T(8,128)S(1)}) fusion(f32[16,256,256]{2,1,0:T(8,128)} %fusion.62, bf16[16,2,128,128]{3,2,1,0:T(8,128)(2,1)S(1)} %gather_fusion, f32[16,128]{1,0:T(8,128)S(1)} %get-tuple-element.371, f32[16,128]{1,0:T(8,128)S(1)} %get-tuple-element.372, f32[128,128]{1,0:T(8,128)S(1)} %add_multiply_fusion.3, ...), kind=kLoop, calls=%fused_computation.31.clone.1 | loop fusion | flops 7602160 | bytes 6373504 | tf_op jit(solution)/shard_map/while/body/eval_jaxpr/reduce_sum | solution.py:71
  357.7 10.9 %add_reduce_fusion.2 = (f32[16]{0:T(128)S(1)}, f32[16,128,128]{2,1,0:T(8,128)S(1)}) fusion(f32[16,256,256]{2,1,0:T(8,128)} %fusion.62, bf16[16,2,128,128]{3,2,1,0:T(8,128)(2,1)S(1)} %gather_fusion, f32[16,128]{1,0:T(8,128)S(1)} %get-tuple-element.371, f32[16,128]{1,0:T(8,128)S(1)} %get-tuple-element.372, f32[128,128]{1,0:T(8,128)S(1)} %add_multiply_fusion.3, ...), kind=kLoop, calls=%fused_computation.31.clone.1 | loop fusion | flops 7602160 | bytes 6373504 | tf_op jit(solution)/shard_map/while/body/eval_jaxpr/reduce_sum | solution.py:71
  376.3 10.9 %add_reduce_fusion.2 = (f32[16]{0:T(128)S(1)}, f32[16,128,128]{2,1,0:T(8,128)S(1)}) fusion(f32[16,256,256]{2,1,0:T(8,128)} %fusion.62, bf16[16,2,128,128]{3,2,1,0:T(8,128)(2,1)S(1)} %gather_fusion, f32[16,128]{1,0:T(8,128)S(1)} %get-tuple-element.371, f32[16,128]{1,0:T(8,128)S(1)} %get-tuple-element.372, f32[128,128]{1,0:T(8,128)S(1)} %add_multiply_fusion.3, ...), kind=kLoop, calls=%fused_computation.31.clone.1 | loop fusion | flops 7602160 | bytes 6373504 | tf_op jit(solution)/shard_map/while/body/eval_jaxpr/reduce_sum | solution.py:71
  395.0 10.9 %add_reduce_fusion.2 = (f32[16]{0:T(128)S(1)}, f32[16,128,128]{2,1,0:T(8,128)S(1)}) fusion(f32[16,256,256]{2,1,0:T(8,128)} %fusion.62, bf16[16,2,128,128]{3,2,1,0:T(8,128)(2,1)S(1)} %gather_fusion, f32[16,128]{1,0:T(8,128)S(1)} %get-tuple-element.371, f32[16,128]{1,0:T(8,128)S(1)} %get-tuple-element.372, f32[128,128]{1,0:T(8,128)S(1)} %add_multiply_fusion.3, ...), kind=kLoop, calls=%fused_computation.31.clone.1 | loop fusion | flops 7602160 | bytes 6373504 | tf_op jit(solution)/shard_map/while/body/eval_jaxpr/reduce_sum | solution.py:71
  407.0 14.0 %all-gather = f32[80,2,256]{2,1,0:T(2,128)S(1)} all-gather(f32[10,2,256]{2,1,0:T(2,128)S(1)} %copy.110), channel_id=2, replica_groups=mesh['groups'=2,'dom'=8,'tilt'=2,'rep'=1] {'dom','rep'}, dimensions={0}, use_global_device_ids=true | all-gather | bytes 184320 | tf_op jit(solution)/shard_map/all_gather | solution.py:175
  425.6 4.9 %all-to-all-done.2 = f32[8,24,3]{1,2,0:T(4,128)S(1)} async-done(((f32[8,24,3]{1,2,0:T(4,128)}), f32[8,24,3]{1,2,0:T(4,128)S(1)}, u32[]{:S(2)}, u32[]{:S(2)}) %all-to-all-start.2) | async-done | bytes 2336 | tf_op jit(solution)/shard_map/all_to_all | solution.py:162
  (276 shorter events, 93.5 us)
Async XLA Ops:
  7.2 31.1 %all-to-all-start.1 = ((bf16[8,24,6]{1,2,0:T(8,128)(2,1)}), bf16[8,24,6]{1,2,0:T(8,128)(2,1)S(1)}, u32[]{:S(2)}, u32[]{:S(2)}) async-start(bf16[8,24,6]{1,2,0:T(8,128)(2,1)} %select_convert_fusion), calls=%async_computation.1 | async-start | bytes 32768 | tf_op jit(solution)/shard_map/all_to_all | solution.py:135
  38.3 6.1 %copy-start = (f32[10,2,256]{2,1,0:T(2,128)S(1)}, f32[10,2,256]{2,1,0:T(2,128)}, u32[]{:S(2)}) copy-start(f32[10,2,256]{2,1,0:T(2,128)} %param.15) | copy-start | bytes 61444
  38.3 144.3 %all-to-all-start = ((bf16[8,24,128,128]{2,3,1,0:T(8,128)(2,1)}), bf16[8,24,128,128]{2,3,1,0:T(8,128)(2,1)}, u32[]{:S(2)}, u32[]{:S(2)}) async-start(bf16[8,24,128,128]{2,3,1,0:T(8,128)(2,1)} %broadcast_select_fusion), calls=%async_computation | async-start | bytes 12582912 | tf_op jit(solution)/shard_map/all_to_all | solution.py:134
  421.6 8.9 %all-to-all-start.2 = ((f32[8,24,3]{1,2,0:T(4,128)}), f32[8,24,3]{1,2,0:T(4,128)S(1)}, u32[]{:S(2)}, u32[]{:S(2)}) async-start(f32[8,24,3]{1,2,0:T(4,128)} %copy.105), calls=%async_computation.2 | async-start | bytes 32768 | tf_op jit(solution)/shard_map/all_to_all | solution.py:162
